TPU v7x, 32 devices: a whole 2x2x4 slice. The times are simulated.
32 devices in a mesh: row: 8 (over y, x, core), col: 4 (over z).
Axes of the slice: x: 2, y: 2, z: 4, core: 2. Of those that a mesh axis runs over, the one named last changes fastest.
Arguments:
- sources: float32 [3, 1024, 4096], P(None, 'row', 'col'), may hold values from -32 to 32
- labels: int32 [1024, 4096], P('row', 'col'), may hold values from 0 to 2
Outputs:
- blended: float32 [1024, 4096], P('row', 'col')
- overview_fine: float32 [512, 2048], P('row', 'col')
- overview_mid: float32 [256, 1024], P(None, 'col')
- overview_coarse: float32 [128, 512], P(None, 'col')
All inputs are finite; a program needn't handle non-finite values.
Results may differ from a plain program's by a relative error of at most 0.0001.
Values sent between devices are 32-bit elements; how exact they have to be, the bound alone decides.
A program may use at most 64 MiB of HBM per device.

v0:
```python
import jax
import jax.numpy as jnp
from jax import lax
from jax.sharding import PartitionSpec as P

ITERS = 3


def with_halo(cells, sides, width):
    for axis, dim in sides:
        count = lax.axis_size(axis)
        ends = count - 1
        head = lax.slice_in_dim(cells, 0, width, axis=dim)
        tail = lax.slice_in_dim(cells, cells.shape[dim] - width, cells.shape[dim], axis=dim)
        cells = jnp.concatenate(
            [
                lax.ppermute(tail, axis, [(i, (i + 1) % count) for i in range(ends)]),
                cells,
                lax.ppermute(head, axis, [((i + 1) % count, i) for i in range(ends)]),
            ],
            axis=dim,
        )
    return cells


def stencil_padded(padded, values):
    beside = padded[2:, 1:-1] + padded[:-2, 1:-1]
    beside = beside + padded[1:-1, 2:] + padded[1:-1, :-2]
    return 4.0 * values - beside


def apply_stencil(values):
    padded = with_halo(values, (("row", 0), ("col", 1)), 1)
    return stencil_padded(padded, values)


def average_pool(values):
    return 0.25 * (
        values[0::2, 0::2] + values[1::2, 0::2] + values[0::2, 1::2] + values[1::2, 1::2]
    )


def two_products(residual, applied):
    return lax.psum((jnp.sum(residual * residual), jnp.sum(residual * applied)), ("row", "col"))


def per_device(sources, labels):
    source_pad = with_halo(sources, (("row", 1), ("col", 2)), 1)
    right_side = jnp.zeros(labels.shape, jnp.float32)
    for channel in range(sources.shape[0]):
        stencil_term = stencil_padded(source_pad[channel], sources[channel])
        right_side = right_side + jnp.where(labels == channel, stencil_term, jnp.float32(0.0))
    blended = jnp.zeros(labels.shape, jnp.float32)
    residual = right_side
    applied = apply_stencil(residual)
    norm_now, product = two_products(residual, applied)
    step_size = norm_now / product
    direction = residual
    along = applied
    for iteration in range(ITERS):
        blended = blended + step_size * direction
        residual = residual - step_size * along
        if iteration + 1 < ITERS:
            applied = apply_stencil(residual)
            norm_next, product = two_products(residual, applied)
            beta_ratio = norm_next / norm_now
            step_size = norm_next / (product - beta_ratio * norm_next / step_size)
            direction = residual + beta_ratio * direction
            along = applied + beta_ratio * along
            norm_now = norm_next
    overview_fine = average_pool(blended)
    overview_mid = lax.all_gather(average_pool(overview_fine), "row", axis=0, tiled=True)
    overview_coarse = average_pool(overview_mid)
    return (blended, overview_fine, overview_mid, overview_coarse)


def solution(mesh):
    return jax.shard_map(
        per_device,
        mesh=mesh,
        in_specs=(P(None, "row", "col"), P("row", "col")),
        out_specs=(P("row", "col"), P("row", "col"), P(None, "col"), P(None, "col")),
        check_vma=False,
    )
```

profile of v0, /device:TPU:0, one launch (start us, length us, event | category | flops | bytes accessed | tf_op | source)
XLA Modules:
  0.0 258.3 jit_solution(15594699302834477659)
XLA Ops:
  0.6 1.0 fusion.23
  1.6 2.4 collective-permute-start
  4.0 1.3 collective-permute-start.1
  5.3 3.9 %collective-permute-done.1 = f32[3,1,1024]{2,1,0:T(1,128)S(1)} collective-permute-done((f32[3,1,1024]{2,1,0:T(1,128)S(1)}, f32[3,1,1024]{2,1,0:T(1,128)S(1)}, u32[]{:S(2)}, u32[]{:S(2)}) %collective-permute-start.1) | collective-permute-done | bytes 12320 | tf_op jit(solution)/shard_map/ppermute | solution.py:19
  9.2 1.6 pad_maximum_fusion
  10.8 0.1 fusion.22
  10.9 1.3 collective-permute-start.3
  12.2 5.2 %collective-permute-start.2 = (f32[3,130,1]{2,1,0:T(8,128)S(1)}, f32[3,130,1]{2,1,0:T(8,128)}, u32[]{:S(2)}, u32[]{:S(2)}) collective-permute-start(f32[3,130,1]{2,1,0:T(8,128)S(1)} %get-tuple-element.20), channel_id=1, source_target_pairs={{0,1},{1,2},{2,3},{4,5},{5,6},{6,7},{8,9},{9,10},{10,11},{12,13},{... | collective-permute-start | bytes 4688 | tf_op jit(solution)/shard_map/ppermute | solution.py:17
  17.5 2.0 collective-permute-done.3
  19.5 1.6 collective-permute-done.2
  21.1 1.8 concatenate.55
  22.9 0.0 copy-start
  23.0 0.1 slice_bitcast_fusion.2
  23.1 1.3 copy-done
  24.3 0.1 copy-done.2
  24.4 1.4 fusion.16
  25.9 3.2 %collective-permute-start.5 = (f32[1,1024]{1,0:T(1,128)S(1)}, f32[1,1024]{1,0:T(1,128)S(1)}, u32[]{:S(2)}, u32[]{:S(2)}) collective-permute-start(f32[1,1024]{1,0:T(1,128)S(1)} %get-tuple-element.33), channel_id=1, source_target_pairs={{0,4},{4,8},{8,12},{12,16},{16,20},{20,24},{24,28},{1,5},{5,9},{9,... | collective-permute-start | bytes 12296 | tf_op jit(solution)/shard_map/ppermute | solution.py:17
  29.1 1.3 collective-permute-start.4
  30.4 2.4 collective-permute-done.4
  32.8 0.1 pad_maximum_fusion.33
  32.9 1.3 collective-permute-start.6
  34.2 5.1 %collective-permute-start.7 = (f32[130,1]{1,0:T(8,128)S(1)}, f32[130,1]{1,0:T(8,128)S(1)}, u32[]{:S(2)}, u32[]{:S(2)}) collective-permute-start(f32[130,1]{1,0:T(8,128)S(1)} %get-tuple-element.28), channel_id=1, source_target_pairs={{0,1},{1,2},{2,3},{4,5},{5,6},{6,7},{8,9},{9,10},{10,11},{12,13},{... | collective-permute-start | bytes 1568 | tf_op jit(solution)/shard_map/ppermute | solution.py:17
  39.3 0.3 collective-permute-done.6
  39.7 1.6 collective-permute-done.7
  41.3 1.0 multiply_reduce_fusion.3
  42.2 43.9 %all-reduce.2 = (f32[]{:T(128)}, f32[]{:T(128)}) all-reduce(f32[]{:T(128)} %get-tuple-element.9, f32[]{:T(128)} %get-tuple-element.8), channel_id=1, replica_groups=mesh['row'=8,'col'=4] {'row','col'}, use_global_device_ids=true, to_apply=%region_1.2 | all-reduce | flops 2 | bytes 16 | tf_op jit(solution)/shard_map/psum | solution.py:44
  87.5 0.4 multiply_subtract_fusion.1
  87.9 1.3 collective-permute-start.9
  89.2 1.3 collective-permute-start.8
  90.5 4.3 %collective-permute-done.8 = f32[1,1024]{1,0:T(1,128)S(1)} collective-permute-done((f32[1,1024]{1,0:T(1,128)S(1)}, f32[1,1024]{1,0:T(1,128)S(1)}, u32[]{:S(2)}, u32[]{:S(2)}) %collective-permute-start.8) | collective-permute-done | bytes 4128 | tf_op jit(solution)/shard_map/ppermute | solution.py:19
  94.7 0.1 pad_maximum_fusion.30
  94.8 1.3 collective-permute-start.10
  96.1 4.5 %collective-permute-start.11 = (f32[130,1]{1,0:T(8,128)S(1)}, f32[130,1]{1,0:T(8,128)S(1)}, u32[]{:S(2)}, u32[]{:S(2)}) collective-permute-start(f32[130,1]{1,0:T(8,128)S(1)} %get-tuple-element.26), channel_id=1, source_target_pairs={{0,1},{1,2},{2,3},{4,5},{5,6},{6,7},{8,9},{9,10},{10,11},{12,13},{... | collective-permute-start | bytes 1568 | tf_op jit(solution)/shard_map/ppermute | solution.py:17
  100.7 0.3 collective-permute-done.10
  101.0 1.6 collective-permute-done.11
  102.6 1.0 multiply_reduce_fusion.1
  103.6 42.7 %all-reduce.1 = (f32[]{:T(128)}, f32[]{:T(128)}) all-reduce(f32[]{:T(128)} %get-tuple-element.7, f32[]{:T(128)} %get-tuple-element.6), channel_id=1, replica_groups=mesh['row'=8,'col'=4] {'row','col'}, use_global_device_ids=true, to_apply=%region_5.6 | all-reduce | flops 2 | bytes 16 | tf_op jit(solution)/shard_map/psum | solution.py:44
  151.0 0.7 multiply_subtract_fusion
  151.7 1.3 collective-permute-start.13
  153.0 1.3 collective-permute-start.12
  154.3 4.3 %collective-permute-done.12 = f32[1,1024]{1,0:T(1,128)S(1)} collective-permute-done((f32[1,1024]{1,0:T(1,128)S(1)}, f32[1,1024]{1,0:T(1,128)S(1)}, u32[]{:S(2)}, u32[]{:S(2)}) %collective-permute-start.12) | collective-permute-done | bytes 4128 | tf_op jit(solution)/shard_map/ppermute | solution.py:19
  158.6 0.1 pad_maximum_fusion.27
  158.6 1.3 collective-permute-start.14
  159.9 4.5 %collective-permute-start.15 = (f32[130,1]{1,0:T(8,128)S(1)}, f32[130,1]{1,0:T(8,128)S(1)}, u32[]{:S(2)}, u32[]{:S(2)}) collective-permute-start(f32[130,1]{1,0:T(8,128)S(1)} %get-tuple-element.24), channel_id=1, source_target_pairs={{0,1},{1,2},{2,3},{4,5},{5,6},{6,7},{8,9},{9,10},{10,11},{12,13},{... | collective-permute-start | bytes 1568 | tf_op jit(solution)/shard_map/ppermute | solution.py:17
  164.5 0.3 collective-permute-done.14
  164.8 1.6 collective-permute-done.15
  166.4 1.0 fusion.3
  167.4 42.5 %all-reduce = (f32[]{:T(128)}, f32[]{:T(128)}) all-reduce(f32[]{:T(128)} %get-tuple-element.5, f32[]{:T(128)} %get-tuple-element.4), channel_id=1, replica_groups=mesh['row'=8,'col'=4] {'row','col'}, use_global_device_ids=true, to_apply=%region_9.10 | all-reduce | flops 2 | bytes 16 | tf_op jit(solution)/shard_map/psum | solution.py:44
  213.9 0.8 multiply_add_fusion
  214.8 4.5 %slice.235 = f32[64,512]{1,0:T(8,128)S(1)} slice(f32[128,1024]{1,0:T(8,128)S(1)} %multiply_add_fusion), slice={[1:128:2], [1:1024:2]} | slice | bytes 262144 | tf_op jit(solution)/shard_map/slice | solution.py:39
  219.3 4.5 %slice.234 = f32[64,512]{1,0:T(8,128)S(1)} slice(f32[128,1024]{1,0:T(8,128)S(1)} %multiply_add_fusion), slice={[0:128:2], [1:1024:2]} | slice | bytes 262144 | tf_op jit(solution)/shard_map/slice | solution.py:39
  223.8 4.5 %slice.233 = f32[64,512]{1,0:T(8,128)S(1)} slice(f32[128,1024]{1,0:T(8,128)S(1)} %multiply_add_fusion), slice={[1:128:2], [0:1024:2]} | slice | bytes 262144 | tf_op jit(solution)/shard_map/slice | solution.py:39
  228.3 4.5 %slice.232 = f32[64,512]{1,0:T(8,128)S(1)} slice(f32[128,1024]{1,0:T(8,128)S(1)} %multiply_add_fusion), slice={[0:128:2], [0:1024:2]} | slice | bytes 262144 | tf_op jit(solution)/shard_map/slice | solution.py:39
  232.9 1.2 slice.239
  234.1 1.2 slice.238
  235.2 1.1 slice.237
  236.4 1.2 slice.236
  237.5 10.5 %all_gather.3 = f32[256,256]{1,0:T(8,128)S(1)} all-gather(f32[32,256]{1,0:T(8,128)S(1)} %add_multiply_fusion.2), channel_id=1, replica_groups=mesh['row'=8,'col'=4] {'row'}, dimensions={0}, use_global_device_ids=true | all-gather | bytes 294912 | tf_op jit(solution)/shard_map/all_gather | solution.py:72
  248.0 2.2 slice.243
  250.2 2.2 slice.242
  252.5 2.2 slice.241
  254.7 2.2 slice.240
  256.9 0.6 add_multiply_fusion.1
  257.6 0.7 copy.7
  (14 shorter events, 0.1 us)
Async XLA Ops:
  1.6 3.7 %collective-permute-start = (f32[3,1,1024]{2,1,0:T(1,128)S(1)}, f32[3,1,1024]{2,1,0:T(1,128)S(1)}, u32[]{:S(2)}, u32[]{:S(2)}) collective-permute-start(f32[3,1,1024]{2,1,0:T(1,128)S(1)} %get-tuple-element.21), channel_id=1, source_target_pairs={{0,4},{4,8},{8,12},{12,16},{16,20},{20,24},{24,28},{1,5},{5,9},{9,... | collective-permute-start | bytes 36872 | tf_op jit(solution)/shard_map/ppermute | solution.py:17
  4.0 5.2 %collective-permute-start.1 = (f32[3,1,1024]{2,1,0:T(1,128)S(1)}, f32[3,1,1024]{2,1,0:T(1,128)S(1)}, u32[]{:S(2)}, u32[]{:S(2)}) collective-permute-start(f32[3,1,1024]{2,1,0:T(1,128)S(1)} %get-tuple-element.22), channel_id=1, source_target_pairs={{4,0},{8,4},{12,8},{16,12},{20,16},{24,20},{28,24},{5,1},{9,5},{13... | collective-permute-start | bytes 36872 | tf_op jit(solution)/shard_map/ppermute | solution.py:19
  10.9 8.6 %collective-permute-start.3 = (f32[3,130,1]{2,1,0:T(8,128)S(1)}, f32[3,130,1]{2,1,0:T(8,128)}, u32[]{:S(2)}, u32[]{:S(2)}) collective-permute-start(f32[3,130,1]{2,1,0:T(8,128)S(1)} %get-tuple-element.19), channel_id=1, source_target_pairs={{1,0},{2,1},{3,2},{5,4},{6,5},{7,6},{9,8},{10,9},{11,10},{13,12},{... | collective-permute-start | bytes 4688 | tf_op jit(solution)/shard_map/ppermute | solution.py:19
  12.2 8.9 %collective-permute-start.2 = (f32[3,130,1]{2,1,0:T(8,128)S(1)}, f32[3,130,1]{2,1,0:T(8,128)}, u32[]{:S(2)}, u32[]{:S(2)}) collective-permute-start(f32[3,130,1]{2,1,0:T(8,128)S(1)} %get-tuple-element.20), channel_id=1, source_target_pairs={{0,1},{1,2},{2,3},{4,5},{5,6},{6,7},{8,9},{9,10},{10,11},{12,13},{... | collective-permute-start | bytes 4688 | tf_op jit(solution)/shard_map/ppermute | solution.py:17
  22.9 1.4 copy-start
  22.9 1.5 copy-start.2
  25.9 4.5 %collective-permute-start.5 = (f32[1,1024]{1,0:T(1,128)S(1)}, f32[1,1024]{1,0:T(1,128)S(1)}, u32[]{:S(2)}, u32[]{:S(2)}) collective-permute-start(f32[1,1024]{1,0:T(1,128)S(1)} %get-tuple-element.33), channel_id=1, source_target_pairs={{0,4},{4,8},{8,12},{12,16},{16,20},{20,24},{24,28},{1,5},{5,9},{9,... | collective-permute-start | bytes 12296 | tf_op jit(solution)/shard_map/ppermute | solution.py:17
  29.1 3.7 %collective-permute-start.4 = (f32[1,1024]{1,0:T(1,128)S(1)}, f32[1,1024]{1,0:T(1,128)S(1)}, u32[]{:S(2)}, u32[]{:S(2)}) collective-permute-start(f32[1,1024]{1,0:T(1,128)S(1)} %get-tuple-element.34), channel_id=1, source_target_pairs={{4,0},{8,4},{12,8},{16,12},{20,16},{24,20},{28,24},{5,1},{9,5},{13... | collective-permute-start | bytes 12296 | tf_op jit(solution)/shard_map/ppermute | solution.py:19
  32.9 6.8 %collective-permute-start.6 = (f32[130,1]{1,0:T(8,128)S(1)}, f32[130,1]{1,0:T(8,128)S(1)}, u32[]{:S(2)}, u32[]{:S(2)}) collective-permute-start(f32[130,1]{1,0:T(8,128)S(1)} %get-tuple-element.27), channel_id=1, source_target_pairs={{1,0},{2,1},{3,2},{5,4},{6,5},{7,6},{9,8},{10,9},{11,10},{13,12},{... | collective-permute-start | bytes 1568 | tf_op jit(solution)/shard_map/ppermute | solution.py:19
  34.2 7.1 %collective-permute-start.7 = (f32[130,1]{1,0:T(8,128)S(1)}, f32[130,1]{1,0:T(8,128)S(1)}, u32[]{:S(2)}, u32[]{:S(2)}) collective-permute-start(f32[130,1]{1,0:T(8,128)S(1)} %get-tuple-element.28), channel_id=1, source_target_pairs={{0,1},{1,2},{2,3},{4,5},{5,6},{6,7},{8,9},{9,10},{10,11},{12,13},{... | collective-permute-start | bytes 1568 | tf_op jit(solution)/shard_map/ppermute | solution.py:17
  87.9 2.6 %collective-permute-start.9 = (f32[1,1024]{1,0:T(1,128)S(1)}, f32[1,1024]{1,0:T(1,128)S(1)}, u32[]{:S(2)}, u32[]{:S(2)}) collective-permute-start(f32[1,1024]{1,0:T(1,128)S(1)} %get-tuple-element.31), channel_id=1, source_target_pairs={{0,4},{4,8},{8,12},{12,16},{16,20},{20,24},{24,28},{1,5},{5,9},{9,... | collective-permute-start | bytes 12296 | tf_op jit(solution)/shard_map/ppermute | solution.py:17
  89.2 5.6 %collective-permute-start.8 = (f32[1,1024]{1,0:T(1,128)S(1)}, f32[1,1024]{1,0:T(1,128)S(1)}, u32[]{:S(2)}, u32[]{:S(2)}) collective-permute-start(f32[1,1024]{1,0:T(1,128)S(1)} %get-tuple-element.32), channel_id=1, source_target_pairs={{4,0},{8,4},{12,8},{16,12},{20,16},{24,20},{28,24},{5,1},{9,5},{13... | collective-permute-start | bytes 12296 | tf_op jit(solution)/shard_map/ppermute | solution.py:19
  94.8 6.2 %collective-permute-start.10 = (f32[130,1]{1,0:T(8,128)S(1)}, f32[130,1]{1,0:T(8,128)S(1)}, u32[]{:S(2)}, u32[]{:S(2)}) collective-permute-start(f32[130,1]{1,0:T(8,128)S(1)} %get-tuple-element.25), channel_id=1, source_target_pairs={{1,0},{2,1},{3,2},{5,4},{6,5},{7,6},{9,8},{10,9},{11,10},{13,12},{... | collective-permute-start | bytes 1568 | tf_op jit(solution)/shard_map/ppermute | solution.py:19
  96.1 6.5 %collective-permute-start.11 = (f32[130,1]{1,0:T(8,128)S(1)}, f32[130,1]{1,0:T(8,128)S(1)}, u32[]{:S(2)}, u32[]{:S(2)}) collective-permute-start(f32[130,1]{1,0:T(8,128)S(1)} %get-tuple-element.26), channel_id=1, source_target_pairs={{0,1},{1,2},{2,3},{4,5},{5,6},{6,7},{8,9},{9,10},{10,11},{12,13},{... | collective-permute-start | bytes 1568 | tf_op jit(solution)/shard_map/ppermute | solution.py:17
  151.7 2.6 %collective-permute-start.13 = (f32[1,1024]{1,0:T(1,128)S(1)}, f32[1,1024]{1,0:T(1,128)S(1)}, u32[]{:S(2)}, u32[]{:S(2)}) collective-permute-start(f32[1,1024]{1,0:T(1,128)S(1)} %get-tuple-element.29), channel_id=1, source_target_pairs={{0,4},{4,8},{8,12},{12,16},{16,20},{20,24},{24,28},{1,5},{5,9},{9,... | collective-permute-start | bytes 12296 | tf_op jit(solution)/shard_map/ppermute | solution.py:17
  153.0 5.6 %collective-permute-start.12 = (f32[1,1024]{1,0:T(1,128)S(1)}, f32[1,1024]{1,0:T(1,128)S(1)}, u32[]{:S(2)}, u32[]{:S(2)}) collective-permute-start(f32[1,1024]{1,0:T(1,128)S(1)} %get-tuple-element.30), channel_id=1, source_target_pairs={{4,0},{8,4},{12,8},{16,12},{20,16},{24,20},{28,24},{5,1},{9,5},{13... | collective-permute-start | bytes 12296 | tf_op jit(solution)/shard_map/ppermute | solution.py:19
  158.6 6.2 %collective-permute-start.14 = (f32[130,1]{1,0:T(8,128)S(1)}, f32[130,1]{1,0:T(8,128)S(1)}, u32[]{:S(2)}, u32[]{:S(2)}) collective-permute-start(f32[130,1]{1,0:T(8,128)S(1)} %get-tuple-element.23), channel_id=1, source_target_pairs={{1,0},{2,1},{3,2},{5,4},{6,5},{7,6},{9,8},{10,9},{11,10},{13,12},{... | collective-permute-start | bytes 1568 | tf_op jit(solution)/shard_map/ppermute | solution.py:19
  159.9 6.5 %collective-permute-start.15 = (f32[130,1]{1,0:T(8,128)S(1)}, f32[130,1]{1,0:T(8,128)S(1)}, u32[]{:S(2)}, u32[]{:S(2)}) collective-permute-start(f32[130,1]{1,0:T(8,128)S(1)} %get-tuple-element.24), channel_id=1, source_target_pairs={{0,1},{1,2},{2,3},{4,5},{5,6},{6,7},{8,9},{9,10},{10,11},{12,13},{... | collective-permute-start | bytes 1568 | tf_op jit(solution)/shard_map/ppermute | solution.py:17
  214.7 43.5 %copy-start.1 = (f32[128,1024]{1,0:T(8,128)}, f32[128,1024]{1,0:T(8,128)S(1)}, u32[]{:S(2)}) copy-start(f32[128,1024]{1,0:T(8,128)S(1)} %multiply_add_fusion) | copy-start | bytes 1572868
  232.9 25.4 %copy-start.3 = (f32[64,512]{1,0:T(8,128)}, f32[64,512]{1,0:T(8,128)S(1)}, u32[]{:S(2)}) copy-start(f32[64,512]{1,0:T(8,128)S(1)} %add_multiply_fusion) | copy-start | bytes 393220
where the time goes:
time: 259 us; the launch traced here: 258 us
  blocking collectives  140 us (54%)
  starting transfers between devices  38 us (15%)
  local copies, waits for them, and re-layouts  36.7 us (14%)
  waiting for transfers between devices  24.2 us (9%)
  between operations  10.9 us (4%)
  other arithmetic  8.85 us (3%)
    psum x3, blocking collectives, two_products(): lax.psum((jnp.sum(residual * residual), jnp.sum(residual * applied)), ('r...  129 us
    ppermute x8, starting transfers between devices, with_halo(): lax.ppermute(tail, axis, [(i, (i + 1) % count) for i in range(ends)])  27.7 us
    ppermute x8, waiting for transfers between devices, with_halo(): lax.ppermute(head, axis, [((i + 1) % count, i) for i in range(ends)])  17.8 us
    all_gather x1, blocking collectives, per_device(): lax.all_gather(average_pool(overview_fine), 'row', axis=0, tiled=True)  10.5 us
    ppermute x8, starting transfers between devices, with_halo(): lax.ppermute(head, axis, [((i + 1) % count, i) for i in range(ends)])  10.3 us
    slice x3, local copies, waits for them, and re-layouts, average_pool(): values[0::2, 0::2] + values[1::2, 0::2] + values[0::2, 1::2]  7.89 us
    slice x3, local copies, waits for them, and re-layouts, average_pool(): values[0::2, 1::2]  7.89 us
    slice x3, local copies, waits for them, and re-layouts, average_pool(): values[1::2, 1::2]  7.89 us
  transfers between devices with their start and end apart: 16, of which 12 were waited for; matrix products, arithmetic and copies ran while one was open for 0% of the time, Pallas kernels for 0%

commit v1 on v0

v1 whole, which is shorter than its diff:
```python
import functools

import jax
import jax.numpy as jnp
from jax import lax
from jax.experimental import pallas as pl
from jax.experimental.pallas import tpu as pltpu
from jax.sharding import PartitionSpec as P

ITERS = 3
MESH = pl.DeviceIdType.MESH
HALO = 4
TOP = 16
SIDES = ((-1, 0), (1, 0), (0, -1), (0, 1), (-1, -1), (-1, 1), (1, -1), (1, 1))


def neighbour_sum(ref, index, start, mid, width):
    above = ref[index + (pl.ds(pl.multiple_of(start - 8, 8), 8), slice(None))]
    below = ref[index + (pl.ds(pl.multiple_of(start + 8, 8), 8), slice(None))]
    sub = lax.broadcasted_iota(jnp.int32, mid.shape, 0)
    up = pltpu.roll(jnp.where(sub == 7, above, mid), 1, axis=0)
    down = pltpu.roll(jnp.where(sub == 0, below, mid), 7, axis=0)
    left = pltpu.roll(mid, 1, axis=1)
    right = pltpu.roll(mid, width - 1, axis=1)
    return (up + down) + (left + right)


def fold_lanes(strip, cols):
    total = strip[:, 0:128]
    for tile in range(1, cols // 128):
        total = total + strip[:, tile * 128:(tile + 1) * 128]
    return total


def quadratic(left, right, moments, shift):
    total = None
    for i, a in enumerate(left):
        for j, b in enumerate(right):
            term = a * b * moments[i + j + shift]
            total = term if total is None else total + term
    return total


def padded_sum(a, b):
    if len(a) < len(b):
        a, b = b, a
    return [x + b[i] if i < len(b) else x for i, x in enumerate(a)]


def coefficients(moments):
    residual = [jnp.ones_like(moments[0])]
    direction = residual
    solution_coords = [jnp.zeros_like(moments[0])]
    norm_now = moments[0]
    for iteration in range(ITERS):
        applied_dot = 4.0 * (
            quadratic(direction, direction, moments, 0)
            - quadratic(direction, direction, moments, 1)
        )
        step = norm_now / applied_dot
        solution_coords = padded_sum(solution_coords, [step * d for d in direction])
        if iteration + 1 < ITERS:
            moved = [-4.0 * step * d for d in direction]
            residual = padded_sum(residual, moved)
            residual = padded_sum(residual, [jnp.zeros_like(step)] + [-m for m in moved])
            norm_next = quadratic(residual, residual, moments, 0)
            ratio = norm_next / norm_now
            direction = padded_sum(residual, [ratio * d for d in direction])
            norm_now = norm_next
    return solution_coords


def kernel(
    n_row, n_col, rows, cols, kinds,
    src_hbm, lab_hbm, blend_ref, fine_ref, mid_ref, coarse_ref,
    src, lab, vec, mask, pack_r, pack_c, got_r, got_c, got_d, moment, mid_all, half,
    load_sem, send_sem, recv_sem, mom_send, mom_recv, mid_send, mid_recv,
):
    width = cols + 128
    n = n_row * n_col
    row, col = lax.axis_index("row"), lax.axis_index("col")
    me = row * n_col + col
    loads = [
        pltpu.make_async_copy(
            src_hbm.at[k], src.at[k, pl.ds(TOP, rows), pl.ds(0, cols)], load_sem.at[k]
        )
        for k in range(kinds)
    ]
    loads.append(
        pltpu.make_async_copy(lab_hbm, lab.at[pl.ds(TOP, rows), pl.ds(0, cols)], load_sem.at[kinds])
    )
    for load in loads:
        load.start()

    barrier = pltpu.get_barrier_semaphore()

    def greet(step, _):
        other = lax.rem(me + step, n)
        pl.semaphore_signal(
            barrier, inc=1, device_id=(other // n_col, lax.rem(other, n_col)), device_id_type=MESH
        )
        return 0

    lax.fori_loop(1, n, greet, 0)

    first_row, last_row = row == 0, row == n_row - 1
    first_col, last_col = col == 0, col == n_col - 1
    quarter = jnp.full((8, width), 0.25, jnp.float32)
    lane = lax.broadcasted_iota(jnp.int32, (8, width), 1)
    off = ((lane >= cols) & (lane < cols + 64) & last_col) | ((lane >= cols + 64) & first_col)
    inside = jnp.where(off, 0.0, quarter)
    mask[0] = jnp.where(first_row, 0.0, inside)
    mask[1] = inside
    mask[2] = jnp.where(last_row, 0.0, inside)
    zero = jnp.zeros((8, width), jnp.float32)
    for which in range(3):
        vec[which, 0:8] = zero
        vec[which, rows + 24:rows + 32] = zero

    for load in loads:
        load.wait()

    for k in range(kinds + 1):
        def edge(rng, lanes):
            if k < kinds:
                return src[k, rng, lanes]
            return lab[rng, lanes].astype(jnp.float32)

        at = slice(HALO * k, HALO * (k + 1))
        pack_r[0, at, :] = edge(pl.ds(TOP, HALO), pl.ds(0, cols))
        pack_r[1, at, :] = edge(pl.ds(TOP + rows - HALO, HALO), pl.ds(0, cols))
    n_pack = HALO * (kinds + 1)
    tile_lane = lax.broadcasted_iota(jnp.int32, (rows, 128), 1)
    packed = jnp.zeros((rows, 128), jnp.float32)
    for k in range(kinds + 1):
        for side in range(2):
            lanes = pl.ds(0 if side == 0 else cols - 128, 128)
            if k < kinds:
                tile = src[k, pl.ds(TOP, rows), lanes]
            else:
                tile = lab[pl.ds(TOP, rows), lanes].astype(jnp.float32)
            target = side * n_pack + HALO * k
            origin = 0 if side == 0 else 128 - HALO
            if (target - origin) % 128:
                tile = pltpu.roll(tile, (target - origin) % 128, axis=1)
            packed = jnp.where((tile_lane >= target) & (tile_lane < target + HALO), tile, packed)
    turned = jnp.transpose(packed)
    pack_c[0] = turned[0:n_pack]
    pack_c[1] = turned[n_pack:2 * n_pack]

    pl.semaphore_wait(barrier, n - 1)

    sends = []
    for i, (dr, dc) in enumerate(SIDES):
        if dc == 0:
            source = pack_r.at[0 if dr < 0 else 1]
            target = got_r.at[1 if dr < 0 else 0]
        elif dr == 0:
            source = pack_c.at[0 if dc < 0 else 1]
            target = got_c.at[1 if dc < 0 else 0]
        else:
            lanes = pl.ds(0 if dc < 0 else cols - 128, 128)
            source = pack_r.at[0 if dr < 0 else 1, :, lanes]
            target = got_d.at[1 if dr < 0 else 0, 1 if dc < 0 else 0]
        there = jnp.logical_and(
            jnp.logical_and(row + dr >= 0, row + dr < n_row),
            jnp.logical_and(col + dc >= 0, col + dc < n_col),
        )
        opposite = SIDES.index((-dr, -dc))
        device = (
            jnp.clip(row + dr, 0, n_row - 1),
            jnp.clip(col + dc, 0, n_col - 1),
        )
        copy = pltpu.make_async_remote_copy(
            src_ref=source, dst_ref=target, send_sem=send_sem.at[i],
            recv_sem=recv_sem.at[opposite], device_id=device, device_id_type=MESH,
        )
        back = pltpu.make_async_remote_copy(
            src_ref=source, dst_ref=got_r.at[0 if dr < 0 else 1] if dc == 0 else (
                got_c.at[0 if dc < 0 else 1] if dr == 0
                else got_d.at[0 if dr < 0 else 1, 0 if dc < 0 else 1]),
            send_sem=send_sem.at[i], recv_sem=recv_sem.at[i],
            device_id=device, device_id_type=MESH,
        )
        sends.append((there, copy, back))
        pl.when(there)(copy.start)
    for there, copy, back in sends:
        pl.when(there)(back.wait_recv)

    halo_lane = lax.broadcasted_iota(jnp.int32, (HALO, 128), 1)
    for side in range(2):
        missing_row = first_row if side == 0 else last_row
        base = TOP - HALO if side == 0 else TOP + rows
        other = TOP - 8 if side == 0 else TOP + rows + HALO
        for k in range(kinds + 1):
            fill = jnp.float32(0.0 if k < kinds else -1.0)
            at = slice(HALO * k, HALO * (k + 1))
            wide = jnp.where(missing_row, fill, got_r[side, at, :])
            right = jnp.where(
                (halo_lane < HALO) & jnp.logical_not(missing_row | last_col),
                got_d[side, 1, at, :], fill)
            corner = jnp.where(
                (halo_lane >= 128 - HALO) & jnp.logical_not(missing_row | first_col),
                got_d[side, 0, at, :], right)
            empty = jnp.full((HALO, width), fill)
            if k < kinds:
                src[k, pl.ds(base, HALO), pl.ds(0, cols)] = wide
                src[k, pl.ds(base, HALO), pl.ds(cols, 128)] = corner
                src[k, pl.ds(other, HALO), :] = empty
            else:
                lab[pl.ds(base, HALO), pl.ds(0, cols)] = wide.astype(jnp.int32)
                lab[pl.ds(base, HALO), pl.ds(cols, 128)] = corner.astype(jnp.int32)
                lab[pl.ds(other, HALO), :] = empty.astype(jnp.int32)
    both = jnp.concatenate(
        [
            got_c[1],
            got_c[0],
            jnp.zeros((128 - 2 * n_pack, rows), jnp.float32),
        ],
        axis=0,
    )
    unturned = jnp.transpose(both)
    for k in range(kinds + 1):
        fill = jnp.float32(0.0 if k < kinds else -1.0)
        right = pltpu.roll(unturned, (-HALO * k) % 128, axis=1)
        left = pltpu.roll(unturned, (128 - HALO - n_pack - HALO * k) % 128, axis=1)
        tile = jnp.where((tile_lane < HALO) & jnp.logical_not(last_col), right, fill)
        tile = jnp.where((tile_lane >= 128 - HALO) & jnp.logical_not(first_col), left, tile)
        if k < kinds:
            src[k, pl.ds(TOP, rows), pl.ds(cols, 128)] = tile
        else:
            lab[pl.ds(TOP, rows), pl.ds(cols, 128)] = tile.astype(jnp.int32)

    groups = rows // 8 + 2

    def right_side(g, _):
        start = pl.multiple_of(g * 8, 8)
        here = lab[pl.ds(start, 8), :]
        total = zero
        for k in range(kinds):
            mid = src[k, pl.ds(start, 8), :]
            term = 4.0 * mid - neighbour_sum(src, (k,), start, mid, width)
            total = jnp.where(here == k, term, total)
        vec[0, pl.ds(start, 8), :] = total
        return 0

    lax.fori_loop(1, groups + 1, right_side, 0)

    def share(g):
        which = jnp.where(g == 1, 0, jnp.where(g == groups, 2, 1))
        return mask[which]

    def apply_to(which):
        def body(g, _):
            start = pl.multiple_of(g * 8, 8)
            mid = vec[which, pl.ds(start, 8), :]
            vec[which + 1, pl.ds(start, 8), :] = share(g) * neighbour_sum(
                vec, (which,), start, mid, width)
            return 0

        lax.fori_loop(1, groups + 1, body, 0)

    for which in range(ITERS - 1):
        apply_to(which)

    def products(g, sums):
        start = pl.multiple_of(g * 8, 8)
        powers = [vec[w, pl.ds(start, 8), :] for w in range(ITERS)]
        powers.append(0.25 * neighbour_sum(vec, (ITERS - 1,), start, powers[-1], width))
        return tuple(
            s + fold_lanes(powers[i // 2] * powers[(i + 1) // 2], cols)
            for i, s in enumerate(sums)
        )

    sums = lax.fori_loop(
        2, groups, products, tuple(jnp.zeros((8, 128), jnp.float32) for _ in range(2 * ITERS)))
    lane1 = lax.broadcasted_iota(jnp.int32, (1, 128), 1)
    mine = jnp.zeros((1, 128), jnp.float32)
    for i, s in enumerate(sums):
        mine = jnp.where(lane1 == i, jnp.sum(s, keepdims=True), mine)
    moment[me] = mine

    def tell(step, _):
        other = lax.rem(me + step, n)
        pltpu.make_async_remote_copy(
            src_ref=moment.at[me], dst_ref=moment.at[me], send_sem=mom_send, recv_sem=mom_recv,
            device_id=(other // n_col, lax.rem(other, n_col)), device_id_type=MESH,
        ).start()
        return 0

    lax.fori_loop(1, n, tell, 0)
    everyone = moment.at[pl.ds(0, n - 1)]
    pltpu.make_async_copy(everyone, everyone, mom_recv).wait()
    total = jnp.sum(moment[...], axis=0)
    moments = [
        jnp.sum(jnp.where(lane1 == i, total, 0.0), axis=1, keepdims=True) for i in range(2 * ITERS)
    ]
    coords = [jnp.broadcast_to(c, (8, cols)) for c in coefficients(moments)]

    def combine(g, _):
        start = pl.multiple_of(g * 8, 8)
        strip = coords[0] * vec[0, pl.ds(start + TOP, 8), pl.ds(0, cols)]
        for w in range(1, ITERS):
            strip = strip + coords[w] * vec[w, pl.ds(start + TOP, 8), pl.ds(0, cols)]
        blend_ref[pl.ds(start, 8), :] = strip
        return 0

    lax.fori_loop(0, rows // 8, combine, 0)

    pool = jnp.where(
        lax.broadcasted_iota(jnp.int32, (256, 128), 0) // 2
        == lax.broadcasted_iota(jnp.int32, (256, 128), 1), 0.25, 0.0).astype(jnp.bfloat16)

    def average(values, slot):
        total = None
        for _ in range(3):
            piece = values.astype(jnp.bfloat16)
            values = values - piece.astype(jnp.float32)
            part = jnp.dot(piece, pool, preferred_element_type=jnp.float32)
            total = part if total is None else total + part
        lines = values.shape[0]
        half[slot, 0:lines, :] = total
        return half[slot, pl.ds(0, lines // 2, stride=2), :] + half[
            slot, pl.ds(1, lines // 2, stride=2), :]

    for tile in range(cols // 256):
        fine_ref[:, tile * 128:(tile + 1) * 128] = average(
            blend_ref[:, tile * 256:(tile + 1) * 256], tile)
    own = pl.ds(pl.multiple_of(row * (rows // 4), 8), rows // 4)
    for tile in range(cols // 512):
        mid_all[own, pl.ds(tile * 128, 128)] = average(
            fine_ref[:, tile * 256:(tile + 1) * 256], tile)

    def spread(step, _):
        other = lax.rem(row + step, n_row)
        pltpu.make_async_remote_copy(
            src_ref=mid_all.at[own], dst_ref=mid_all.at[own], send_sem=mid_send, recv_sem=mid_recv,
            device_id=(other, col), device_id_type=MESH,
        ).start()
        return 0

    lax.fori_loop(1, n_row, spread, 0)
    others = mid_all.at[pl.ds(0, (n_row - 1) * (rows // 4))]
    pltpu.make_async_copy(others, others, mid_recv).wait()
    mid_ref[...] = mid_all[...]
    for tile in range(cols // 1024):
        coarse_ref[:, tile * 128:(tile + 1) * 128] = average(
            mid_all[:, tile * 256:(tile + 1) * 256], tile)

    for there, copy, back in sends:
        pl.when(there)(copy.wait_send)
    pltpu.make_async_copy(everyone, everyone, mom_send).wait()
    pltpu.make_async_copy(others, others, mid_send).wait()


def per_device(n_row, n_col, sources, labels):
    kinds, rows, cols = sources.shape
    n = n_row * n_col
    tall, width = rows + 32, cols + 128
    n_pack = HALO * (kinds + 1)
    f32 = jnp.float32
    vmem = pl.BlockSpec(memory_space=pltpu.VMEM)
    return pl.pallas_call(
        functools.partial(kernel, n_row, n_col, rows, cols, kinds),
        out_shape=(
            jax.ShapeDtypeStruct((rows, cols), f32),
            jax.ShapeDtypeStruct((rows // 2, cols // 2), f32),
            jax.ShapeDtypeStruct((n_row * rows // 4, cols // 4), f32),
            jax.ShapeDtypeStruct((n_row * rows // 8, cols // 8), f32),
        ),
        in_specs=[pl.BlockSpec(memory_space=pl.ANY)] * 2,
        out_specs=(vmem,) * 4,
        scratch_shapes=[
            pltpu.VMEM((kinds, tall, width), f32),
            pltpu.VMEM((tall, width), jnp.int32),
            pltpu.VMEM((ITERS, tall, width), f32),
            pltpu.VMEM((3, 8, width), f32),
            pltpu.VMEM((2, n_pack, cols), f32),
            pltpu.VMEM((2, n_pack, rows), f32),
            pltpu.VMEM((2, n_pack, cols), f32),
            pltpu.VMEM((2, n_pack, rows), f32),
            pltpu.VMEM((2, 2, n_pack, 128), f32),
            pltpu.VMEM((n, 1, 128), f32),
            pltpu.VMEM((n_row * rows // 4, cols // 4), f32),
            pltpu.VMEM((cols // 256, max(rows, n_row * rows // 4), 128), f32),
            pltpu.SemaphoreType.DMA((kinds + 1,)),
            pltpu.SemaphoreType.DMA((8,)),
            pltpu.SemaphoreType.DMA((8,)),
            pltpu.SemaphoreType.DMA,
            pltpu.SemaphoreType.DMA,
            pltpu.SemaphoreType.DMA,
            pltpu.SemaphoreType.DMA,
        ],
        compiler_params=pltpu.CompilerParams(collective_id=0, has_side_effects=True),
    )(sources, labels)


def solution(mesh):
    sizes = dict(mesh.shape)
    return jax.shard_map(
        functools.partial(per_device, sizes["row"], sizes["col"]),
        mesh=mesh,
        in_specs=(P(None, "row", "col"), P("row", "col")),
        out_specs=(P("row", "col"), P("row", "col"), P(None, "col"), P(None, "col")),
        check_vma=False,
    )
```

time: 259 us -> 35.4 us (0.14)
  blocking collectives: 140 us -> 0 us
  starting transfers between devices: 38 us -> 0 us
  local copies, waits for them, and re-layouts: 36.7 us -> 5.79 us
  Pallas kernels: 0 us -> 28.8 us
  waiting for transfers between devices: 24.2 us -> 0 us
  between operations: 10.9 us -> 0.65 us
  other arithmetic: 8.85 us -> 0 us
    psum x3 -> x0, blocking collectives: 129 us -> none  [two_products(): lax.psum((jnp.sum(residual * residual), jnp.sum(residual * applied)), ('r...]
    ppermute x16 -> x0, starting transfers between devices: 38 us -> none  [the longest x8 27.7 us: with_halo(): lax.ppermute(tail, axis, [(i, (i + 1) % count) for i in range(ends)])]
    slice x17 -> x0, local copies, waits for them, and re-layouts: 32.7 us -> none  [the longest x3 7.89 us: average_pool(): values[0::2, 0::2] + values[1::2, 0::2] + values[0::2, 1::2]]
    pallas_call x0 -> x1, Pallas kernels: none -> 28.8 us  [per_device(): pl.pallas_call(functools.partial(kernel, n_row, n_col, rows, cols, kinds)...]
    ppermute x16 -> x0, waiting for transfers between devices: 24.2 us -> none  [the longest x8 17.8 us: with_halo(): lax.ppermute(head, axis, [((i + 1) % count, i) for i in range(ends)])]
    all_gather x1 -> x0, blocking collectives: 10.5 us -> none  [per_device(): lax.all_gather(average_pool(overview_fine), 'row', axis=0, tiled=True)]
    unnamed x9 -> x6, local copies, waits for them, and re-layouts: 2.08 us -> 5.79 us
    reduce_sum x3 -> x0, other arithmetic: 2.97 us -> none  [two_products(): jnp.sum(residual * applied)]
  transfers between devices with their start and end apart: 16 -> 0, of which waited for: 12 -> 0; matrix products, arithmetic and copies ran while one was open for 0% -> 0% of each run, Pallas kernels for 0% -> 0%
where the time goes in v1:
time: 35.4 us; the launch traced here: 35.2 us
  Pallas kernels  28.8 us (81%)
  local copies, waits for them, and re-layouts  5.79 us (16%)
  between operations  0.65 us (2%)
    pallas_call x1, Pallas kernels, per_device(): pl.pallas_call(functools.partial(kernel, n_row, n_col, rows, cols, kinds)...  28.8 us
    unnamed x6, local copies, waits for them, and re-layouts  5.79 us

profile of v1, /device:TPU:0, one launch (start us, length us, event | category | flops | bytes accessed | tf_op | source)
XLA Modules:
  0.0 35.2 jit_solution(4298845678434543721)
XLA Ops:
  0.6 28.8 %shard_map.57 = (f32[128,1024]{1,0:T(8,128)}, f32[64,512]{1,0:T(8,128)}, f32[256,256]{1,0:T(8,128)}, f32[128,128]{1,0:T(8,128)}) custom-call(f32[3,128,1024]{2,1,0:T(8,128)} %src_hbm.1, s32[128,1024]{1,0:T(8,128)} %lab_hbm.1), custom_call_target="tpu_custom_call" | custom-call | tf_op jit(solution)/shard_map/pallas_call | solution.py:363
  29.4 0.0 copy-start
  29.4 1.9 %copy.10 = f32[128,1024]{1,0:T(8,128)} copy(f32[128,1024]{1,0:T(8,128)} %get-tuple-element.8) | data formatting | bytes 1048576
  31.3 1.6 %copy.11 = f32[64,512]{1,0:T(8,128)} copy(f32[64,512]{1,0:T(8,128)} %get-tuple-element.9) | data formatting | bytes 262144
  32.9 1.7 %copy.12 = f32[256,256]{1,0:T(8,128)} copy(f32[256,256]{1,0:T(8,128)} %get-tuple-element.10) | data formatting | bytes 524288
  34.6 0.0 copy-done
  34.6 0.6 %copy.13 = f32[128,128]{1,0:T(8,128)} copy(f32[128,128]{1,0:T(8,128)S(1)} %copy-done) | data formatting | bytes 131072
Async XLA Ops:
  29.4 5.2 %copy-start = (f32[128,128]{1,0:T(8,128)S(1)}, f32[128,128]{1,0:T(8,128)}, u32[]{:S(2)}) copy-start(f32[128,128]{1,0:T(8,128)} %get-tuple-element.11) | copy-start | bytes 196612

commit v2 on v1

--- a/solution.py
+++ b/solution.py
@@ -70,11 +70,32 @@
     return solution_coords
 
 
-def kernel(
+def pooled(values, half, slot, pool, stride):
+    total = None
+    for _ in range(3):
+        piece = values.astype(jnp.bfloat16)
+        values = values - piece.astype(jnp.float32)
+        part = jnp.dot(piece, pool, preferred_element_type=jnp.float32)
+        total = part if total is None else total + part
+    lines = values.shape[0]
+    half[slot, 0:lines, :] = total
+    result = half[slot, pl.ds(0, lines // stride, stride=stride), :]
+    for line in range(1, stride):
+        result = result + half[slot, pl.ds(line, lines // stride, stride=stride), :]
+    return result
+
+
+def pool_matrix(stride):
+    shape = (128 * stride, 128)
+    source, target = (lax.broadcasted_iota(jnp.int32, shape, d) for d in range(2))
+    return jnp.where(source // stride == target, 1.0 / (stride * stride), 0.0).astype(jnp.bfloat16)
+
+
+def gather_kernel(
     n_row, n_col, rows, cols, kinds,
-    src_hbm, lab_hbm, blend_ref, fine_ref, mid_ref, coarse_ref,
-    src, lab, vec, mask, pack_r, pack_c, got_r, got_c, got_d, moment, mid_all, half,
-    load_sem, send_sem, recv_sem, mom_send, mom_recv, mid_send, mid_recv,
+    src_hbm, lab_hbm, vec, mids, coord_ref,
+    src, lab, mask, pack_r, pack_c, got_r, got_c, got_d, moment, half,
+    load_sem, send_sem, recv_sem, mom_send, mom_recv, mid_send, mid_recv, fwd_send, fwd_recv,
 ):
     width = cols + 128
     n = n_row * n_col
@@ -94,14 +115,25 @@
 
     barrier = pltpu.get_barrier_semaphore()
 
-    def greet(step, _):
-        other = lax.rem(me + step, n)
-        pl.semaphore_signal(
-            barrier, inc=1, device_id=(other // n_col, lax.rem(other, n_col)), device_id_type=MESH
-        )
-        return 0
-
-    lax.fori_loop(1, n, greet, 0)
+    columns = [col]
+    for _ in range(n_col - 1):
+        columns.append(jnp.where(columns[-1] + 1 == n_col, 0, columns[-1] + 1))
+
+    def for_all_others(act):
+        for c in columns[1:]:
+            act(row, c)
+
+        def body(step, _):
+            r = row + step
+            r = jnp.where(r >= n_row, r - n_row, r)
+            for c in columns:
+                act(r, c)
+            return 0
+
+        lax.fori_loop(1, n_row, body, 0)
+
+    for_all_others(lambda r, c: pl.semaphore_signal(
+        barrier, inc=1, device_id=(r, c), device_id_type=MESH))
 
     first_row, last_row = row == 0, row == n_row - 1
     first_col, last_col = col == 0, col == n_col - 1
@@ -244,7 +276,7 @@
         vec[0, pl.ds(start, 8), :] = total
         return 0
 
-    lax.fori_loop(1, groups + 1, right_side, 0)
+    lax.fori_loop(1, groups + 1, right_side, 0, unroll=2)
 
     def share(g):
         which = jnp.where(g == 1, 0, jnp.where(g == groups, 2, 1))
@@ -258,10 +290,44 @@
                 vec, (which,), start, mid, width)
             return 0
 
-        lax.fori_loop(1, groups + 1, body, 0)
-
+        lax.fori_loop(1, groups + 1, body, 0, unroll=3)
+
+    chips = n_row // 2
+    partner = row + 1 - 2 * lax.rem(row, 2)
+    quad = rows // 4
+    pool = pool_matrix(4)
+
+    def block(w, owner):
+        return mids.at[w, pl.ds(pl.multiple_of(owner * quad, 8), quad)]
+
+    def peer(step):
+        other = row + 2 * step
+        return jnp.where(other >= n_row, other - n_row, other)
+
+    def hand(w, owner, target, send, recv):
+        return pltpu.make_async_remote_copy(
+            src_ref=block(w, owner), dst_ref=block(w, owner), send_sem=send, recv_sem=recv,
+            device_id=(target, col), device_id_type=MESH)
+
+    def gather(w):
+        for tile in range(cols // 512):
+            mids[w, pl.ds(pl.multiple_of(row * quad, 8), quad), pl.ds(tile * 128, 128)] = pooled(
+                vec[w, pl.ds(TOP, rows), pl.ds(tile * 512, 512)], half,
+                w * (cols // 512) + tile, pool, 4)
+        hops = [
+            hand(w, row, peer(step), mid_send.at[w, step], mid_recv.at[w, step])
+            for step in range(1, chips)
+        ]
+        hops.append(hand(w, row, partner, mid_send.at[w, 0], mid_recv.at[w, 0]))
+        for hop in hops:
+            hop.start()
+        return hops
+
+    hops = []
     for which in range(ITERS - 1):
+        hops += gather(which)
         apply_to(which)
+    hops += gather(ITERS - 1)
 
     def products(g, sums):
         start = pl.multiple_of(g * 8, 8)
@@ -273,84 +339,94 @@
         )
 
     sums = lax.fori_loop(
-        2, groups, products, tuple(jnp.zeros((8, 128), jnp.float32) for _ in range(2 * ITERS)))
+        2, groups, products, tuple(jnp.zeros((8, 128), jnp.float32) for _ in range(2 * ITERS)), unroll=2)
     lane1 = lax.broadcasted_iota(jnp.int32, (1, 128), 1)
     mine = jnp.zeros((1, 128), jnp.float32)
     for i, s in enumerate(sums):
         mine = jnp.where(lane1 == i, jnp.sum(s, keepdims=True), mine)
     moment[me] = mine
 
-    def tell(step, _):
-        other = lax.rem(me + step, n)
-        pltpu.make_async_remote_copy(
-            src_ref=moment.at[me], dst_ref=moment.at[me], send_sem=mom_send, recv_sem=mom_recv,
-            device_id=(other // n_col, lax.rem(other, n_col)), device_id_type=MESH,
-        ).start()
-        return 0
-
-    lax.fori_loop(1, n, tell, 0)
+    for_all_others(lambda r, c: pltpu.make_async_remote_copy(
+        src_ref=moment.at[me], dst_ref=moment.at[me], send_sem=mom_send, recv_sem=mom_recv,
+        device_id=(r, c), device_id_type=MESH).start())
     everyone = moment.at[pl.ds(0, n - 1)]
     pltpu.make_async_copy(everyone, everyone, mom_recv).wait()
     total = jnp.sum(moment[...], axis=0)
     moments = [
         jnp.sum(jnp.where(lane1 == i, total, 0.0), axis=1, keepdims=True) for i in range(2 * ITERS)
     ]
-    coords = [jnp.broadcast_to(c, (8, cols)) for c in coefficients(moments)]
-
-    def combine(g, _):
-        start = pl.multiple_of(g * 8, 8)
-        strip = coords[0] * vec[0, pl.ds(start + TOP, 8), pl.ds(0, cols)]
-        for w in range(1, ITERS):
-            strip = strip + coords[w] * vec[w, pl.ds(start + TOP, 8), pl.ds(0, cols)]
-        blend_ref[pl.ds(start, 8), :] = strip
-        return 0
-
-    lax.fori_loop(0, rows // 8, combine, 0)
-
-    pool = jnp.where(
-        lax.broadcasted_iota(jnp.int32, (256, 128), 0) // 2
-        == lax.broadcasted_iota(jnp.int32, (256, 128), 1), 0.25, 0.0).astype(jnp.bfloat16)
-
-    def average(values, slot):
-        total = None
-        for _ in range(3):
-            piece = values.astype(jnp.bfloat16)
-            values = values - piece.astype(jnp.float32)
-            part = jnp.dot(piece, pool, preferred_element_type=jnp.float32)
-            total = part if total is None else total + part
-        lines = values.shape[0]
-        half[slot, 0:lines, :] = total
-        return half[slot, pl.ds(0, lines // 2, stride=2), :] + half[
-            slot, pl.ds(1, lines // 2, stride=2), :]
-
-    for tile in range(cols // 256):
-        fine_ref[:, tile * 128:(tile + 1) * 128] = average(
-            blend_ref[:, tile * 256:(tile + 1) * 256], tile)
-    own = pl.ds(pl.multiple_of(row * (rows // 4), 8), rows // 4)
-    for tile in range(cols // 512):
-        mid_all[own, pl.ds(tile * 128, 128)] = average(
-            fine_ref[:, tile * 256:(tile + 1) * 256], tile)
-
-    def spread(step, _):
-        other = lax.rem(row + step, n_row)
-        pltpu.make_async_remote_copy(
-            src_ref=mid_all.at[own], dst_ref=mid_all.at[own], send_sem=mid_send, recv_sem=mid_recv,
-            device_id=(other, col), device_id_type=MESH,
-        ).start()
-        return 0
-
-    lax.fori_loop(1, n_row, spread, 0)
-    others = mid_all.at[pl.ds(0, (n_row - 1) * (rows // 4))]
-    pltpu.make_async_copy(others, others, mid_recv).wait()
-    mid_ref[...] = mid_all[...]
-    for tile in range(cols // 1024):
-        coarse_ref[:, tile * 128:(tile + 1) * 128] = average(
-            mid_all[:, tile * 256:(tile + 1) * 256], tile)
-
+    for w, c in enumerate(coefficients(moments)):
+        coord_ref[w] = jnp.broadcast_to(c, (8, 128))
+
+    def source_of(step):
+        other = row - 2 * step
+        return jnp.where(other < 0, other + n_row, other)
+
+    def other_core(owner):
+        return owner + 1 - 2 * lax.rem(owner, 2)
+
+    forwards = []
+    for w in range(ITERS):
+        for step in range(1, chips):
+            owner = source_of(step)
+            hand(w, owner, partner, mid_send.at[w, step], mid_recv.at[w, step]).wait_recv()
+            forward = hand(w, owner, partner, fwd_send.at[w, step], fwd_recv.at[w, step])
+            forward.start()
+            forwards.append(forward)
+    for w in range(ITERS):
+        hand(w, partner, partner, mid_send.at[w, 0], mid_recv.at[w, 0]).wait_recv()
+        for step in range(1, chips):
+            hand(w, other_core(source_of(step)), partner,
+                 fwd_send.at[w, step], fwd_recv.at[w, step]).wait_recv()
+    for hop in hops:
+        hop.wait_send()
+    for forward in forwards:
+        forward.wait_send()
     for there, copy, back in sends:
         pl.when(there)(copy.wait_send)
     pltpu.make_async_copy(everyone, everyone, mom_send).wait()
-    pltpu.make_async_copy(others, others, mid_send).wait()
+
+
+def finish_kernel(
+    rows, cols, vec, mids, coord_ref, blend_out, fine_out, mid_out, coarse_out,
+    blend, fine, mid, coarse, half, out_sem,
+):
+    pool = pool_matrix(2)
+
+    def leave(slot, source, target):
+        copy = pltpu.make_async_copy(source, target, out_sem.at[slot])
+        copy.start()
+        return copy
+
+    def combine(source, target, lines, lanes, first):
+        coords = [jnp.concatenate([coord_ref[w]] * (lanes // 128), axis=1) for w in range(ITERS)]
+
+        def body(g, _):
+            start = pl.multiple_of(g * 8, 8)
+            strip = None
+            for w in range(ITERS):
+                term = coords[w] * source[w, pl.ds(start + first, 8), pl.ds(0, lanes)]
+                strip = term if strip is None else strip + term
+            target[pl.ds(start, 8), :] = strip
+            return 0
+
+        lax.fori_loop(0, lines // 8, body, 0, unroll=4)
+
+    combine(vec, blend, rows, cols, TOP)
+    copies = [leave(0, blend, blend_out)]
+    tall, wide = mid.shape
+    combine(mids, mid, tall, wide, 0)
+    copies.append(leave(1, mid, mid_out))
+    for tile in range(cols // 256):
+        fine[:, tile * 128:(tile + 1) * 128] = pooled(
+            blend[:, tile * 256:(tile + 1) * 256], half, tile, pool, 2)
+    copies.append(leave(2, fine, fine_out))
+    for tile in range(wide // 256):
+        coarse[:, tile * 128:(tile + 1) * 128] = pooled(
+            mid[:, tile * 256:(tile + 1) * 256], half, cols // 256 + tile, pool, 2)
+    copies.append(leave(3, coarse, coarse_out))
+    for copy in copies:
+        copy.wait()
 
 
 def per_device(n_row, n_col, sources, labels):
@@ -360,20 +436,23 @@
     n_pack = HALO * (kinds + 1)
     f32 = jnp.float32
     vmem = pl.BlockSpec(memory_space=pltpu.VMEM)
-    return pl.pallas_call(
-        functools.partial(kernel, n_row, n_col, rows, cols, kinds),
+    hbm = pl.BlockSpec(memory_space=pltpu.HBM)
+    mid_shape = (n_row * rows // 4, cols // 4)
+    coarse_shape = (n_row * rows // 8, cols // 8)
+    chips = n_row // 2
+    dma = pltpu.SemaphoreType.DMA
+    vec, mids, coords = pl.pallas_call(
+        functools.partial(gather_kernel, n_row, n_col, rows, cols, kinds),
         out_shape=(
-            jax.ShapeDtypeStruct((rows, cols), f32),
-            jax.ShapeDtypeStruct((rows // 2, cols // 2), f32),
-            jax.ShapeDtypeStruct((n_row * rows // 4, cols // 4), f32),
-            jax.ShapeDtypeStruct((n_row * rows // 8, cols // 8), f32),
+            jax.ShapeDtypeStruct((ITERS, tall, width), f32),
+            jax.ShapeDtypeStruct((ITERS,) + mid_shape, f32),
+            jax.ShapeDtypeStruct((ITERS, 8, 128), f32),
         ),
-        in_specs=[pl.BlockSpec(memory_space=pl.ANY)] * 2,
-        out_specs=(vmem,) * 4,
+        in_specs=[hbm] * 2,
+        out_specs=(vmem,) * 3,
         scratch_shapes=[
             pltpu.VMEM((kinds, tall, width), f32),
             pltpu.VMEM((tall, width), jnp.int32),
-            pltpu.VMEM((ITERS, tall, width), f32),
             pltpu.VMEM((3, 8, width), f32),
             pltpu.VMEM((2, n_pack, cols), f32),
             pltpu.VMEM((2, n_pack, rows), f32),
@@ -381,18 +460,43 @@
             pltpu.VMEM((2, n_pack, rows), f32),
             pltpu.VMEM((2, 2, n_pack, 128), f32),
             pltpu.VMEM((n, 1, 128), f32),
-            pltpu.VMEM((n_row * rows // 4, cols // 4), f32),
-            pltpu.VMEM((cols // 256, max(rows, n_row * rows // 4), 128), f32),
-            pltpu.SemaphoreType.DMA((kinds + 1,)),
-            pltpu.SemaphoreType.DMA((8,)),
-            pltpu.SemaphoreType.DMA((8,)),
-            pltpu.SemaphoreType.DMA,
-            pltpu.SemaphoreType.DMA,
-            pltpu.SemaphoreType.DMA,
-            pltpu.SemaphoreType.DMA,
+            pltpu.VMEM((ITERS * (cols // 512), rows, 128), f32),
+            dma((kinds + 1,)),
+            dma((8,)),
+            dma((8,)),
+            dma,
+            dma,
+            dma((ITERS, chips)),
+            dma((ITERS, chips)),
+            dma((ITERS, chips)),
+            dma((ITERS, chips)),
         ],
-        compiler_params=pltpu.CompilerParams(collective_id=0, has_side_effects=True),
-    )(sources, labels)
+        compiler_params=pltpu.CompilerParams(
+            collective_id=0, has_side_effects=True, vmem_limit_bytes=20 * 2**20),
+    )(
+        pltpu.with_memory_space_constraint(sources, pltpu.HBM),
+        pltpu.with_memory_space_constraint(labels, pltpu.HBM),
+    )
+    return pl.pallas_call(
+        functools.partial(finish_kernel, rows, cols),
+        out_shape=(
+            jax.ShapeDtypeStruct((rows, cols), f32),
+            jax.ShapeDtypeStruct((rows // 2, cols // 2), f32),
+            jax.ShapeDtypeStruct(mid_shape, f32),
+            jax.ShapeDtypeStruct(coarse_shape, f32),
+        ),
+        in_specs=[vmem] * 3,
+        out_specs=(hbm,) * 4,
+        scratch_shapes=[
+            pltpu.VMEM((rows, cols), f32),
+            pltpu.VMEM((rows // 2, cols // 2), f32),
+            pltpu.VMEM(mid_shape, f32),
+            pltpu.VMEM(coarse_shape, f32),
+            pltpu.VMEM((cols // 256 + cols // 1024, max(rows, mid_shape[0]), 128), f32),
+            dma((4,)),
+        ],
+        compiler_params=pltpu.CompilerParams(vmem_limit_bytes=20 * 2**20),
+    )(vec, mids, coords)
 
 
 def solution(mesh):

time: 35.4 us -> 25.2 us (0.71)
  local copies, waits for them, and re-layouts: 5.79 us -> 0 us
  Pallas kernels: 28.8 us -> 24.4 us
    unnamed x6 -> x0, local copies, waits for them, and re-layouts: 5.79 us -> none
    pallas_call x1 -> x2, Pallas kernels: 28.8 us -> 24.4 us  [the longest x1 22.9 us: per_device(): pl.pallas_call(functools.partial(gather_kernel, n_row, n_col, rows, cols,...]
where the time goes in v2:
time: 25.2 us; the launch traced here: 25 us
  Pallas kernels  24.4 us (97%)
  between operations  0.64 us (3%)
    pallas_call x1, Pallas kernels, per_device(): pl.pallas_call(functools.partial(gather_kernel, n_row, n_col, rows, cols,...  22.9 us
    pallas_call x1, Pallas kernels, per_device(): pl.pallas_call(functools.partial(finish_kernel, rows, cols), out_shape=(j...  1.45 us

profile of v2, /device:TPU:0, one launch (start us, length us, event | category | flops | bytes accessed | tf_op | source)
XLA Modules:
  0.0 25.0 jit_solution(15414807251798386685)
XLA Ops:
  0.6 22.9 %shard_map.57 = (f32[3,160,1152]{2,1,0:T(8,128)S(1)}, f32[3,256,256]{2,1,0:T(8,128)S(1)}, f32[3,8,128]{2,1,0:T(8,128)S(1)}) custom-call(f32[3,128,1024]{2,1,0:T(8,128)} %src_hbm.1, s32[128,1024]{1,0:T(8,128)} %lab_hbm.1), custom_call_target="tpu_custom_call" | custom-call | tf_op jit(solution)/shard_map/pallas_call | solution.py:444
  23.6 1.4 %shard_map.58 = (f32[128,1024]{1,0:T(8,128)}, f32[64,512]{1,0:T(8,128)}, f32[256,256]{1,0:T(8,128)}, f32[128,128]{1,0:T(8,128)}) custom-call(f32[3,160,1152]{2,1,0:T(8,128)S(1)} %get-tuple-element.7.vec, f32[3,256,256]{2,1,0:T(8,128)S(1)} %get-tuple-element.8.mids, f32[3,8,128]{2,1,0:T(8,128)S(1)} %get-tuple-element.9.coord_ref), custom_call_target="tpu_custom_call" | custom-call | tf_op jit(solution)/shard_map/pallas_call | solution.py:480

commit v3 on v2

--- a/solution.py
+++ b/solution.py
@@ -94,13 +94,11 @@
 def gather_kernel(
     n_row, n_col, rows, cols, kinds,
     src_hbm, lab_hbm, vec, mids, coord_ref,
-    src, lab, mask, pack_r, pack_c, got_r, got_c, got_d, moment, half,
+    src, lab, mask, pack_r, pack_c, got_r, got_c, got_d, mom_col, mom_row, half,
     load_sem, send_sem, recv_sem, mom_send, mom_recv, mid_send, mid_recv, fwd_send, fwd_recv,
 ):
     width = cols + 128
-    n = n_row * n_col
     row, col = lax.axis_index("row"), lax.axis_index("col")
-    me = row * n_col + col
     loads = [
         pltpu.make_async_copy(
             src_hbm.at[k], src.at[k, pl.ds(TOP, rows), pl.ds(0, cols)], load_sem.at[k]
@@ -115,25 +113,32 @@
 
     barrier = pltpu.get_barrier_semaphore()
 
-    columns = [col]
-    for _ in range(n_col - 1):
-        columns.append(jnp.where(columns[-1] + 1 == n_col, 0, columns[-1] + 1))
-
-    def for_all_others(act):
-        for c in columns[1:]:
-            act(row, c)
-
-        def body(step, _):
-            r = row + step
-            r = jnp.where(r >= n_row, r - n_row, r)
-            for c in columns:
-                act(r, c)
-            return 0
-
-        lax.fori_loop(1, n_row, body, 0)
-
-    for_all_others(lambda r, c: pl.semaphore_signal(
-        barrier, inc=1, device_id=(r, c), device_id_type=MESH))
+    def ring(place, count):
+        places = []
+        for _ in range(count - 1):
+            place = jnp.where(place + 1 == count, 0, place + 1)
+            places.append(place)
+        return places
+
+    col_peers = [(row, c) for c in ring(col, n_col)]
+    row_peers = [(r, col) for r in ring(row, n_row)]
+
+    def greet(device):
+        pl.semaphore_signal(barrier, inc=1, device_id=device, device_id_type=MESH)
+
+    for dr in (-1, 1):
+        for dc in (-1, 1):
+            there = jnp.logical_and(
+                jnp.logical_and(row + dr >= 0, row + dr < n_row),
+                jnp.logical_and(col + dc >= 0, col + dc < n_col),
+            )
+            device = (jnp.clip(row + dr, 0, n_row - 1), jnp.clip(col + dc, 0, n_col - 1))
+            pl.when(there)(functools.partial(greet, device))
+    for device in col_peers + row_peers:
+        greet(device)
+    corners = (
+        jnp.where(row == 0, 0, 1) + jnp.where(row == n_row - 1, 0, 1)
+    ) * (jnp.where(col == 0, 0, 1) + jnp.where(col == n_col - 1, 0, 1))
 
     first_row, last_row = row == 0, row == n_row - 1
     first_col, last_col = col == 0, col == n_col - 1
@@ -180,7 +185,7 @@
     pack_c[0] = turned[0:n_pack]
     pack_c[1] = turned[n_pack:2 * n_pack]
 
-    pl.semaphore_wait(barrier, n - 1)
+    pl.semaphore_wait(barrier, n_row + n_col - 2 + corners)
 
     sends = []
     for i, (dr, dc) in enumerate(SIDES):
@@ -327,7 +332,6 @@
     for which in range(ITERS - 1):
         hops += gather(which)
         apply_to(which)
-    hops += gather(ITERS - 1)
 
     def products(g, sums):
         start = pl.multiple_of(g * 8, 8)
@@ -344,19 +348,20 @@
     mine = jnp.zeros((1, 128), jnp.float32)
     for i, s in enumerate(sums):
         mine = jnp.where(lane1 == i, jnp.sum(s, keepdims=True), mine)
-    moment[me] = mine
-
-    for_all_others(lambda r, c: pltpu.make_async_remote_copy(
-        src_ref=moment.at[me], dst_ref=moment.at[me], send_sem=mom_send, recv_sem=mom_recv,
-        device_id=(r, c), device_id_type=MESH).start())
-    everyone = moment.at[pl.ds(0, n - 1)]
-    pltpu.make_async_copy(everyone, everyone, mom_recv).wait()
-    total = jnp.sum(moment[...], axis=0)
-    moments = [
-        jnp.sum(jnp.where(lane1 == i, total, 0.0), axis=1, keepdims=True) for i in range(2 * ITERS)
-    ]
-    for w, c in enumerate(coefficients(moments)):
-        coord_ref[w] = jnp.broadcast_to(c, (8, 128))
+
+    def share_out(buffer, slot, value, peers, send, recv):
+        buffer[slot] = value
+        for device in peers:
+            pltpu.make_async_remote_copy(
+                src_ref=buffer.at[slot], dst_ref=buffer.at[slot], send_sem=send, recv_sem=recv,
+                device_id=device, device_id_type=MESH).start()
+        return buffer.at[pl.ds(0, len(peers))]
+
+    col_rest = share_out(mom_col, col, mine, col_peers, mom_send.at[0], mom_recv.at[0])
+    hops += gather(ITERS - 1)
+    pltpu.make_async_copy(col_rest, col_rest, mom_recv.at[0]).wait()
+    part = jnp.sum(mom_col[...], axis=0)
+    row_rest = share_out(mom_row, row, part, row_peers, mom_send.at[1], mom_recv.at[1])
 
     def source_of(step):
         other = row - 2 * step
@@ -378,13 +383,21 @@
         for step in range(1, chips):
             hand(w, other_core(source_of(step)), partner,
                  fwd_send.at[w, step], fwd_recv.at[w, step]).wait_recv()
+    pltpu.make_async_copy(row_rest, row_rest, mom_recv.at[1]).wait()
+    total = jnp.sum(mom_row[...], axis=0)
+    moments = [
+        jnp.sum(jnp.where(lane1 == i, total, 0.0), axis=1, keepdims=True) for i in range(2 * ITERS)
+    ]
+    for w, c in enumerate(coefficients(moments)):
+        coord_ref[w] = jnp.broadcast_to(c, (8, 128))
     for hop in hops:
         hop.wait_send()
     for forward in forwards:
         forward.wait_send()
     for there, copy, back in sends:
         pl.when(there)(copy.wait_send)
-    pltpu.make_async_copy(everyone, everyone, mom_send).wait()
+    pltpu.make_async_copy(col_rest, col_rest, mom_send.at[0]).wait()
+    pltpu.make_async_copy(row_rest, row_rest, mom_send.at[1]).wait()
 
 
 def finish_kernel(
@@ -431,7 +444,6 @@
 
 def per_device(n_row, n_col, sources, labels):
     kinds, rows, cols = sources.shape
-    n = n_row * n_col
     tall, width = rows + 32, cols + 128
     n_pack = HALO * (kinds + 1)
     f32 = jnp.float32
@@ -459,13 +471,14 @@
             pltpu.VMEM((2, n_pack, cols), f32),
             pltpu.VMEM((2, n_pack, rows), f32),
             pltpu.VMEM((2, 2, n_pack, 128), f32),
-            pltpu.VMEM((n, 1, 128), f32),
+            pltpu.VMEM((n_col, 1, 128), f32),
+            pltpu.VMEM((n_row, 1, 128), f32),
             pltpu.VMEM((ITERS * (cols // 512), rows, 128), f32),
             dma((kinds + 1,)),
             dma((8,)),
             dma((8,)),
-            dma,
-            dma,
+            dma((2,)),
+            dma((2,)),
             dma((ITERS, chips)),
             dma((ITERS, chips)),
             dma((ITERS, chips)),

time: 25.2 us -> 25.8 us (1.024)
  Pallas kernels: 24.4 us -> 25 us
    pallas_call x1, Pallas kernels: 22.9 us -> 23.6 us  [per_device(): pl.pallas_call(functools.partial(gather_kernel, n_row, n_col, rows, cols,...]
where the time goes in v3:
time: 25.8 us; the launch traced here: 25.7 us
  Pallas kernels  25 us (97%)
  between operations  0.64 us (2%)
    pallas_call x1, Pallas kernels, per_device(): pl.pallas_call(functools.partial(gather_kernel, n_row, n_col, rows, cols,...  23.6 us
    pallas_call x1, Pallas kernels, per_device(): pl.pallas_call(functools.partial(finish_kernel, rows, cols), out_shape=(j...  1.45 us

profile of v3, /device:TPU:0, one launch (start us, length us, event | category | flops | bytes accessed | tf_op | source)
XLA Modules:
  0.0 25.7 jit_solution(15257833754987497511)
XLA Ops:
  0.6 23.6 %shard_map.57 = (f32[3,160,1152]{2,1,0:T(8,128)S(1)}, f32[3,256,256]{2,1,0:T(8,128)S(1)}, f32[3,8,128]{2,1,0:T(8,128)S(1)}) custom-call(f32[3,128,1024]{2,1,0:T(8,128)} %src_hbm.1, s32[128,1024]{1,0:T(8,128)} %lab_hbm.1), custom_call_target="tpu_custom_call" | custom-call | tf_op jit(solution)/shard_map/pallas_call | solution.py:456
  24.2 1.4 %shard_map.58 = (f32[128,1024]{1,0:T(8,128)}, f32[64,512]{1,0:T(8,128)}, f32[256,256]{1,0:T(8,128)}, f32[128,128]{1,0:T(8,128)}) custom-call(f32[3,160,1152]{2,1,0:T(8,128)S(1)} %get-tuple-element.7.vec, f32[3,256,256]{2,1,0:T(8,128)S(1)} %get-tuple-element.8.mids, f32[3,8,128]{2,1,0:T(8,128)S(1)} %get-tuple-element.9.coord_ref), custom_call_target="tpu_custom_call" | custom-call | tf_op jit(solution)/shard_map/pallas_call | solution.py:493

commit v4 on v2

--- a/solution.py
+++ b/solution.py
@@ -14,9 +14,16 @@
 SIDES = ((-1, 0), (1, 0), (0, -1), (0, 1), (-1, -1), (-1, 1), (1, -1), (1, 1))
 
 
-def neighbour_sum(ref, index, start, mid, width):
-    above = ref[index + (pl.ds(pl.multiple_of(start - 8, 8), 8), slice(None))]
-    below = ref[index + (pl.ds(pl.multiple_of(start + 8, 8), 8), slice(None))]
+def load_strip(ref, index, start, lanes):
+    start = start if isinstance(start, int) else pl.multiple_of(start, 8)
+    parts = [ref[index + (pl.ds(start, 8), pl.ds(first, size))] for first, size in lanes]
+    return parts[0] if len(parts) == 1 else jnp.concatenate(parts, axis=1)
+
+
+def neighbour_sum(ref, index, start, lanes, mid):
+    width = mid.shape[1]
+    above = load_strip(ref, index, start - 8, lanes)
+    below = load_strip(ref, index, start + 8, lanes)
     sub = lax.broadcasted_iota(jnp.int32, mid.shape, 0)
     up = pltpu.roll(jnp.where(sub == 7, above, mid), 1, axis=0)
     down = pltpu.roll(jnp.where(sub == 0, below, mid), 7, axis=0)
@@ -180,6 +187,54 @@
     pack_c[0] = turned[0:n_pack]
     pack_c[1] = turned[n_pack:2 * n_pack]
 
+    groups = rows // 8 + 2
+    whole = ((0, width),)
+    around = ((cols - 128, 256), (0, 128))
+
+    def right_side(start, lanes):
+        here = load_strip(lab, (), start, lanes)
+        total = jnp.zeros(here.shape, jnp.float32)
+        for k in range(kinds):
+            mid = load_strip(src, (k,), start, lanes)
+            term = 4.0 * mid - neighbour_sum(src, (k,), start, lanes, mid)
+            total = jnp.where(here == k, term, total)
+        return total
+
+    def stage(which, g, lanes, share):
+        start = g * 8
+        if which == 0:
+            return right_side(start, lanes)
+        mid = load_strip(vec, (which - 1,), start, lanes)
+        return load_strip(mask, (share,), 0, lanes) * neighbour_sum(
+            vec, (which - 1,), start, lanes, mid)
+
+    def inner(which):
+        def body(g, _):
+            vec[which, pl.ds(pl.multiple_of(g * 8, 8), 8), :] = stage(which, g, whole, 1)
+            return 0
+
+        lax.fori_loop(2, groups, body, 0, unroll=2)
+
+    edge_lane = lax.broadcasted_iota(jnp.int32, (8, 128), 1)
+
+    def frame(which):
+        for g, share in ((1, 0), (2, 1), (groups - 1, 1), (groups, 2)):
+            vec[which, pl.ds(g * 8, 8), :] = stage(which, g, whole, share)
+
+        def body(g, _):
+            lines = pl.ds(pl.multiple_of(g * 8, 8), 8)
+            new = stage(which, g, around, 1)
+            last = vec[which, lines, pl.ds(cols - 128, 128)]
+            first = vec[which, lines, pl.ds(0, 128)]
+            vec[which, lines, pl.ds(cols - 128, 128)] = jnp.where(
+                edge_lane >= 64, new[:, 0:128], last)
+            vec[which, lines, pl.ds(cols, 128)] = new[:, 128:256]
+            vec[which, lines, pl.ds(0, 128)] = jnp.where(edge_lane < 64, new[:, 256:384], first)
+            return 0
+
+        lax.fori_loop(3, groups - 1, body, 0, unroll=2)
+
+    inner(0)
     pl.semaphore_wait(barrier, n - 1)
 
     sends = []
@@ -216,6 +271,9 @@
         )
         sends.append((there, copy, back))
         pl.when(there)(copy.start)
+    for which in range(1, ITERS):
+        inner(which)
+
     for there, copy, back in sends:
         pl.when(there)(back.wait_recv)
 
@@ -263,35 +321,6 @@
         else:
             lab[pl.ds(TOP, rows), pl.ds(cols, 128)] = tile.astype(jnp.int32)
 
-    groups = rows // 8 + 2
-
-    def right_side(g, _):
-        start = pl.multiple_of(g * 8, 8)
-        here = lab[pl.ds(start, 8), :]
-        total = zero
-        for k in range(kinds):
-            mid = src[k, pl.ds(start, 8), :]
-            term = 4.0 * mid - neighbour_sum(src, (k,), start, mid, width)
-            total = jnp.where(here == k, term, total)
-        vec[0, pl.ds(start, 8), :] = total
-        return 0
-
-    lax.fori_loop(1, groups + 1, right_side, 0, unroll=2)
-
-    def share(g):
-        which = jnp.where(g == 1, 0, jnp.where(g == groups, 2, 1))
-        return mask[which]
-
-    def apply_to(which):
-        def body(g, _):
-            start = pl.multiple_of(g * 8, 8)
-            mid = vec[which, pl.ds(start, 8), :]
-            vec[which + 1, pl.ds(start, 8), :] = share(g) * neighbour_sum(
-                vec, (which,), start, mid, width)
-            return 0
-
-        lax.fori_loop(1, groups + 1, body, 0, unroll=3)
-
     chips = n_row // 2
     partner = row + 1 - 2 * lax.rem(row, 2)
     quad = rows // 4
@@ -324,15 +353,15 @@
         return hops
 
     hops = []
+    frame(0)
     for which in range(ITERS - 1):
         hops += gather(which)
-        apply_to(which)
-    hops += gather(ITERS - 1)
+        frame(which + 1)
 
     def products(g, sums):
         start = pl.multiple_of(g * 8, 8)
         powers = [vec[w, pl.ds(start, 8), :] for w in range(ITERS)]
-        powers.append(0.25 * neighbour_sum(vec, (ITERS - 1,), start, powers[-1], width))
+        powers.append(0.25 * neighbour_sum(vec, (ITERS - 1,), start, whole, powers[-1]))
         return tuple(
             s + fold_lanes(powers[i // 2] * powers[(i + 1) // 2], cols)
             for i, s in enumerate(sums)
@@ -349,6 +378,7 @@
     for_all_others(lambda r, c: pltpu.make_async_remote_copy(
         src_ref=moment.at[me], dst_ref=moment.at[me], send_sem=mom_send, recv_sem=mom_recv,
         device_id=(r, c), device_id_type=MESH).start())
+    hops += gather(ITERS - 1)
     everyone = moment.at[pl.ds(0, n - 1)]
     pltpu.make_async_copy(everyone, everyone, mom_recv).wait()
     total = jnp.sum(moment[...], axis=0)

time: 25.2 us -> 25 us (level)
  no operation moved by 1% of the time
where the time goes in v4:
time: 25 us; the launch traced here: 24.8 us
  Pallas kernels  24.2 us (97%)
  between operations  0.64 us (3%)
    pallas_call x1, Pallas kernels, per_device(): pl.pallas_call(functools.partial(gather_kernel, n_row, n_col, rows, cols,...  22.7 us
    pallas_call x1, Pallas kernels, per_device(): pl.pallas_call(functools.partial(finish_kernel, rows, cols), out_shape=(j...  1.44 us

profile of v4, /device:TPU:0, one launch (start us, length us, event | category | flops | bytes accessed | tf_op | source)
XLA Modules:
  0.0 24.8 jit_solution(12651590104172584685)
XLA Ops:
  0.6 22.7 %shard_map.57 = (f32[3,160,1152]{2,1,0:T(8,128)S(1)}, f32[3,256,256]{2,1,0:T(8,128)S(1)}, f32[3,8,128]{2,1,0:T(8,128)S(1)}) custom-call(f32[3,128,1024]{2,1,0:T(8,128)} %src_hbm.1, s32[128,1024]{1,0:T(8,128)} %lab_hbm.1), custom_call_target="tpu_custom_call" | custom-call | tf_op jit(solution)/shard_map/pallas_call | solution.py:474
  23.4 1.4 %shard_map.58 = (f32[128,1024]{1,0:T(8,128)}, f32[64,512]{1,0:T(8,128)}, f32[256,256]{1,0:T(8,128)}, f32[128,128]{1,0:T(8,128)}) custom-call(f32[3,160,1152]{2,1,0:T(8,128)S(1)} %get-tuple-element.7.vec, f32[3,256,256]{2,1,0:T(8,128)S(1)} %get-tuple-element.8.mids, f32[3,8,128]{2,1,0:T(8,128)S(1)} %get-tuple-element.9.coord_ref), custom_call_target="tpu_custom_call" | custom-call | tf_op jit(solution)/shard_map/pallas_call | solution.py:510
